TPU v7x, 32 devices: a whole 2x2x4 slice. The times are simulated.
32 devices in a mesh: groups: 2 (over x), dp: 4 (over y, core), fsdp: 4 (over z).
Axes of the slice: x: 2, y: 2, z: 4, core: 2. Of those that a mesh axis runs over, the one named last changes fastest.
Arguments:
- tokens: bfloat16 [4096, 4096], P(('groups', 'dp', 'fsdp')), parts along dimension 0, may hold values from -6 to 6
- up_weight: bfloat16 [4096, 14336], P('fsdp', 'dp'), may hold values from -0.09375 to 0.09375
- first_adapter_factors: bfloat16 [32, 32, 4096], P(('groups', 'dp', 'fsdp')), parts along dimension 0, may hold values from -0.09375 to 0.09375
- second_adapter_factors: bfloat16 [32, 32, 14336], P(('groups', 'dp', 'fsdp')), parts along dimension 0, may hold values from -1 to 1
- counts: int32 [32], P(('groups', 'dp', 'fsdp')), parts along dimension 0, may hold values from 1 to 128, as said below
- output_gradient: bfloat16 [4096, 14336], P(('groups', 'dp', 'fsdp')), parts along dimension 0, may hold values from -6 to 6
Outputs:
- act_out: bfloat16 [4096, 14336], P(('groups', 'dp', 'fsdp')), parts along dimension 0
- grad_a: float32 [32, 32, 4096], P(('groups', 'dp', 'fsdp')), parts along dimension 0
- second_factor_gradient: float32 [32, 32, 14336], P(('groups', 'dp', 'fsdp')), parts along dimension 0
There are 2 independent parts, one for each index of `groups`. A program takes and returns all parts, laid end to end along the dimension named above; an argument that names none is the same for every part. Nothing has to cross between parts.
Inputs may be any that keep to these rules, and one draw needn't show every extreme that they name: counts[d] is the number of live rows of adapter d. For d < 8, counts[d] + counts[d + 8] <= 160; in every draw some such pair has the counts 128 and 32.
All inputs are finite; a program needn't handle non-finite values.
Results may differ from a plain program's by a relative error of at most 0.0058.
Values may be sent and summed in bfloat16 or wider, within the bound.
No kernel may reach another device: no remote copies, remote signals or barrier semaphores. Data moves between devices by JAX's collectives and lax.ppermute only.
A program may use at most 128 MiB of HBM per device.

v0:
```python
import jax
import jax.numpy as jnp
from jax import lax
from jax.sharding import PartitionSpec as P

SLOTS = 128
PAIR_ROWS = 80
LOWRANK_SCALE = 2.0


def partner(x, axis, distance):
    return lax.ppermute(x, axis, [(i, i ^ 1 << distance) for i in range(lax.axis_size(axis))])


def silu_slope(inputs):
    gate_value = jax.nn.sigmoid(inputs)
    return gate_value * (1.0 + inputs * (1.0 - gate_value))


def take_block(rows_all, offset, row_count):
    filler = jnp.zeros((row_count,) + rows_all.shape[1:], rows_all.dtype)
    padded = jnp.concatenate([rows_all, filler], 0)
    return lax.dynamic_slice_in_dim(padded, offset, row_count, 0)


def place_block(rows_kept, block, offset, row_total):
    filler = jnp.zeros((block.shape[0],) + rows_kept.shape[1:], rows_kept.dtype)
    padded = jnp.concatenate([rows_kept, filler], 0)
    placed = lax.dynamic_update_slice_in_dim(padded, block, offset, 0)
    return placed[:row_total]


def per_device(
    tokens, up_weight, first_adapter_factors, second_adapter_factors, counts, output_gradient
):
    down_factor = first_adapter_factors[0]
    up_factor = second_adapter_factors[0]
    slot_total = tokens.shape[0]
    own_count = counts[0]
    live_rows = jnp.arange(slot_total, dtype=jnp.int32)[:, None] < own_count
    spare_rows = SLOTS - PAIR_ROWS
    half_bit = lax.axis_size("dp").bit_length() - 2
    kept_rows = jnp.minimum(own_count, PAIR_ROWS)
    outgoing = take_block(tokens, kept_rows, spare_rows)
    guest = partner(outgoing, "dp", half_bit)
    paired_rows = place_block(tokens[:PAIR_ROWS], guest, kept_rows, PAIR_ROWS)
    dp_total, fsdp_total = (lax.axis_size("dp"), lax.axis_size("fsdp"))
    sliced_rows = lax.all_to_all(paired_rows, "fsdp", split_axis=1, concat_axis=0, tiled=True)
    slice_width = sliced_rows.shape[1]
    all_rows = lax.all_gather(sliced_rows, "dp", axis=0, tiled=True)
    all_rows = all_rows.reshape(dp_total, fsdp_total, PAIR_ROWS, slice_width).swapaxes(0, 1)
    partial_blocks = jnp.dot(
        all_rows.reshape(-1, slice_width), up_weight, preferred_element_type=jnp.float32
    ).astype(jnp.bfloat16)
    blocks = lax.psum_scatter(partial_blocks, "fsdp", scatter_dimension=0, tiled=True)
    paired_base = lax.all_to_all(blocks, "dp", split_axis=0, concat_axis=1, tiled=True)
    returned = partner(take_block(paired_base, kept_rows, spare_rows), "dp", half_bit)
    base_output = place_block(paired_base, returned, kept_rows, SLOTS)
    rank_projection = lax.dot_general(
        tokens, down_factor, (((1,), (1,)), ((), ())), preferred_element_type=jnp.float32
    ).astype(jnp.bfloat16)
    adapter_update = jnp.dot(rank_projection, up_factor, preferred_element_type=jnp.float32)
    hidden_preactivation = base_output.astype(jnp.float32) + LOWRANK_SCALE * adapter_update
    act_out = jnp.where(live_rows, jax.nn.silu(hidden_preactivation), 0.0).astype(jnp.bfloat16)
    grad_pre = jnp.where(
        live_rows, output_gradient.astype(jnp.float32) * silu_slope(hidden_preactivation), 0.0
    ).astype(jnp.bfloat16)
    low_rank_gradient = (
        LOWRANK_SCALE
        * lax.dot_general(
            grad_pre, up_factor, (((1,), (1,)), ((), ())), preferred_element_type=jnp.float32
        )
    ).astype(jnp.bfloat16)
    second_factor_gradient = LOWRANK_SCALE * lax.dot_general(
        rank_projection, grad_pre, (((0,), (0,)), ((), ())), preferred_element_type=jnp.float32
    )
    grad_a = lax.dot_general(
        low_rank_gradient, tokens, (((0,), (0,)), ((), ())), preferred_element_type=jnp.float32
    )
    return (act_out, grad_a[None], second_factor_gradient[None])


def solution(mesh):
    placed = (
        P(("groups", "dp", "fsdp"), None),
        P("fsdp", "dp"),
        P(("groups", "dp", "fsdp"), None, None),
        P(("groups", "dp", "fsdp"), None, None),
        P(("groups", "dp", "fsdp")),
        P(("groups", "dp", "fsdp"), None),
    )
    return jax.shard_map(
        per_device,
        mesh=mesh,
        in_specs=placed,
        out_specs=(
            P(("groups", "dp", "fsdp"), None),
            P(("groups", "dp", "fsdp"), None, None),
            P(("groups", "dp", "fsdp"), None, None),
        ),
        check_vma=False,
    )
```

profile of v0, /device:TPU:0, one launch (start us, length us, event | category | flops | bytes accessed | tf_op | source)
XLA Modules:
  0.0 340.4 jit_solution(10477999457115856074)
XLA Ops:
  7.2 0.0 copy-start
  7.2 0.0 all-gather.2.cloned.1.call-start
  8.0 1.2 pad_dynamic-slice_fusion
  9.1 3.1 collective-permute-start
  12.2 1.4 broadcast_select_fusion
  13.6 7.7 %collective-permute-done = bf16[48,4096]{1,0:T(8,128)(2,1)S(1)} collective-permute-done((bf16[48,4096]{1,0:T(8,128)(2,1)S(1)}, bf16[48,4096]{1,0:T(8,128)(2,1)S(1)}, u32[]{:S(2)}, u32[]{:S(2)}) %collective-permute-start) | collective-permute-done | bytes 393248 | tf_op jit(solution)/shard_map/ppermute | solution.py:12
  21.3 2.3 dynamic_update_slice.6
  23.6 21.0 %all_to_all.38 = bf16[80,4,1024]{2,0,1:T(8,128)(2,1)} all-to-all(bf16[80,4,1024]{2,0,1:T(8,128)(2,1)S(1)} %bitcast.49), channel_id=1, replica_groups=mesh['groups'=2,'dp'=4,'fsdp'=4] {'fsdp'}, dimensions={1} | all-to-all | bytes 1310720 | tf_op jit(solution)/shard_map/all_to_all | solution.py:48
  44.7 0.0 all-gather.2.cloned.1.call-update
  44.7 0.0 reduce-scatter.2.cloned.1.call-start
  44.7 25.2 %all-gather.2.cloned.1.call-done = bf16[1280,1024]{1,0:T(8,128)(2,1)} async-done(((bf16[320,1024]{1,0:T(8,128)(2,1)}), bf16[1280,1024]{1,0:T(8,128)(2,1)}) %all-gather.2.cloned.1.call-update) | async-done | bytes 2621456 | tf_op jit(solution)/shard_map/all_gather | solution.py:50
  69.9 2.1 copy.16
  72.0 14.9 %convolution_convert_fusion = bf16[1280,3584]{1,0:T(8,128)(2,1)} fusion(bf16[1280,1024]{1,0:T(8,128)(2,1)S(1)} %bitcast.46, bf16[1024,3584]{1,0:T(8,128)(2,1)} %param.7), kind=kOutput, calls=%fused_computation.3 | convolution fusion | flops 9399828480 | bytes 19136512 | tf_op jit(solution)/shard_map/dot_general | solution.py:52
  86.9 0.0 reduce-scatter.2.cloned.1.call-update
  86.9 157.2 %reduce-scatter.2.cloned.1.call-done = bf16[320,3584]{1,0:T(8,128)(2,1)} async-done(((bf16[1280,3584]{1,0:T(8,128)(2,1)}), bf16[320,3584]{1,0:T(8,128)(2,1)}) %reduce-scatter.2.cloned.1.call-update) | async-done | bytes 2293776 | tf_op jit(solution)/shard_map/reduce_scatter | solution.py:55
  244.1 31.4 %all_to_all.39 = bf16[4,80,3584]{2,1,0:T(8,128)(2,1)S(1)} all-to-all(bf16[4,80,3584]{2,1,0:T(8,128)(2,1)} %bitcast.50), channel_id=1, replica_groups=mesh['groups'=2,'dp'=4,'fsdp'=4] {'dp'}, dimensions={0} | all-to-all | bytes 4587520 | tf_op jit(solution)/shard_map/all_to_all | solution.py:56
  275.5 0.0 copy-start.1
  275.5 0.0 copy-start.3
  275.5 0.2 copy.19
  275.7 0.4 pad_dynamic-slice_fusion.1
  276.1 0.5 collective-permute-start.1
  276.6 0.1 copy-done.1
  276.7 0.0 copy-done.3
  276.7 0.5 convolution_convert_fusion.1
  277.2 2.1 concatenate.12
  279.3 28.7 %collective-permute-done.1 = bf16[48,14336]{1,0:T(8,128)(2,1)S(1)} collective-permute-done((bf16[48,14336]{1,0:T(8,128)(2,1)S(1)}, bf16[48,14336]{1,0:T(8,128)(2,1)S(1)}, u32[]{:S(2)}, u32[]{:S(2)}) %collective-permute-start.1) | collective-permute-done | bytes 1376288 | tf_op jit(solution)/shard_map/ppermute | solution.py:12
  308.1 9.0 %dynamic_update_slice.7 = bf16[128,14336]{1,0:T(8,128)(2,1)} dynamic-update-slice(bf16[128,14336]{1,0:T(8,128)(2,1)} %concatenate.12, bf16[48,14336]{1,0:T(8,128)(2,1)S(1)} %collective-permute-done.1, s32[]{:T(128)S(6)} %select_n.16, s32[]{:T(128)} %constant.2.clone.1) | dynamic-update-slice | bytes 2752516 | tf_op jit(solution)/shard_map/dynamic_update_slice | solution.py:29
  317.1 0.0 copy-done
  317.1 8.2 %select_convert_fusion = (bf16[128,14336]{1,0:T(8,128)(2,1)S(1)}, bf16[128,14336]{1,0:T(8,128)(2,1)}) fusion(bf16[128,14336]{1,0:T(8,128)(2,1)} %param.11, bf16[128,14336]{1,0:T(8,128)(2,1)} %dynamic_update_slice.7, pred[128]{0:T(512)(128)(4,1)S(1)} %iota_compare_fusion, bf16[128,32]{0,1:T(8,128)(2,1)S(1)} %convolution_convert_fusion.1, ...), kind=kOutput, calls=%fused_computation.4 | convolution fusion | flops 148635648 | bytes 15605888 | tf_op jit(solution)/shard_map/dot_general | solution.py:62
  325.3 0.0 copy-start.2
  325.3 1.8 copy-done.2
  327.1 1.8 fusion
  328.9 4.6 %convolution_bitcast_fusion = f32[1,32,4096]{2,1,0:T(8,128)} fusion(bf16[128,4096]{1,0:T(8,128)(2,1)S(1)} %copy-done.1, bf16[128,14336]{1,0:T(8,128)(2,1)} %copy-done.2, bf16[1,32,14336]{2,1,0:T(8,128)(2,1)S(1)} %copy-done), kind=kOutput, calls=%fused_computation.8 | convolution fusion | flops 151003136 | bytes 6160384 | tf_op jit(solution)/shard_map/dot_general | solution.py:77
  (3 shorter events, 0.1 us)
Async XLA Ops:
  7.2 309.9 %copy-start = (bf16[1,32,14336]{2,1,0:T(8,128)(2,1)S(1)}, bf16[1,32,14336]{2,1,0:T(8,128)(2,1)}, u32[]{:S(2)}) copy-start(bf16[1,32,14336]{2,1,0:T(8,128)(2,1)} %param.9) | copy-start | bytes 2752516
  7.2 62.8 %all-gather.2.cloned.1.call-start = ((), (), s32[]{:S(2)}) async-start(), calls=%async_computation.3 | async-start | bytes 3276800 | tf_op jit(solution)/shard_map/all_gather | solution.py:50
  9.1 12.2 %collective-permute-start = (bf16[48,4096]{1,0:T(8,128)(2,1)S(1)}, bf16[48,4096]{1,0:T(8,128)(2,1)S(1)}, u32[]{:S(2)}, u32[]{:S(2)}) collective-permute-start(bf16[48,4096]{1,0:T(8,128)(2,1)S(1)} %pad_dynamic-slice_fusion), channel_id=1, source_target_pairs={{0,8},{4,12},{8,0},{12,4},{1,9},{5,13},{9,1},{13,5},{2,10},{6,14},... | collective-permute-start | bytes 1179656 | tf_op jit(solution)/shard_map/ppermute | solution.py:12
  44.7 199.4 %reduce-scatter.2.cloned.1.call-start = ((), (), s32[]{:S(2)}) async-start(), calls=%async_computation.4 | async-start | bytes 11468800 | tf_op jit(solution)/shard_map/reduce_scatter | solution.py:55
  275.5 1.2 copy-start.1
  275.5 1.3 copy-start.3
  276.1 31.9 %collective-permute-start.1 = (bf16[48,14336]{1,0:T(8,128)(2,1)S(1)}, bf16[48,14336]{1,0:T(8,128)(2,1)S(1)}, u32[]{:S(2)}, u32[]{:S(2)}) collective-permute-start(bf16[48,14336]{1,0:T(8,128)(2,1)S(1)} %pad_dynamic-slice_fusion.1), channel_id=1, source_target_pairs={{0,8},{4,12},{8,0},{12,4},{1,9},{5,13},{9,1},{13,5},{2,10},{6,14},... | collective-permute-start | bytes 4128776 | tf_op jit(solution)/shard_map/ppermute | solution.py:12
  325.3 1.8 copy-start.2
Sparse Core Ops, SparseCore 0:
  44.8 25.0 all-gather.1
  87.0 157.0 reduce-scatter.1
where the time goes:
time: 341 us; the launch traced here: 340 us
  waiting for transfers between devices  219 us (64%)
  blocking collectives  52.4 us (15%)
  matrix products  30 us (9%)
  local copies, waits for them, and re-layouts  19.3 us (6%)
  between operations  14.8 us (4%)
  starting transfers between devices  3.6 us (1%)
    reduce_scatter x1, waiting for transfers between devices, per_device(): lax.psum_scatter(partial_blocks, 'fsdp', scatter_dimension=0, tiled=True)  157 us
    ppermute x2, waiting for transfers between devices, partner(): lax.ppermute(x, axis, [(i, i ^ 1 << distance) for i in range(lax.axis_siz...  36.5 us
    all_to_all x1, blocking collectives, per_device(): lax.all_to_all(blocks, 'dp', split_axis=0, concat_axis=1, tiled=True)  31.4 us
    all_gather x1, waiting for transfers between devices, per_device(): all_rows = lax.all_gather(sliced_rows, 'dp', axis=0, tiled=True)  25.2 us
    all_to_all x1, blocking collectives, per_device(): lax.all_to_all(paired_rows, 'fsdp', split_axis=1, concat_axis=0, tiled=True)  21 us
    dot_general x1, matrix products, per_device(): jnp.dot(all_rows.reshape(-1, slice_width), up_weight, preferred_element_t...  14.9 us
    dynamic_update_slice x2, local copies, waits for them, and re-layouts, place_block(): placed = lax.dynamic_update_slice_in_dim(padded, block, offset, 0)  11.3 us
    dot_general x1, matrix products, per_device(): jnp.dot(rank_projection, up_factor, preferred_element_type=jnp.float32)  8.18 us
  transfers between devices with their start and end apart: 4, of which 4 were waited for; matrix products, arithmetic and copies ran while one was open for 1% of the time, Pallas kernels for 0%

commit v1 on v0

--- a/solution.py
+++ b/solution.py
@@ -6,6 +6,9 @@
 SLOTS = 128
 PAIR_ROWS = 80
 LOWRANK_SCALE = 2.0
+test_sides_over_axis = lambda block_here, axis_tag: jnp.concatenate(
+    lax.all_to_all(jnp.stack(jnp.split(block_here, lax.axis_size(axis_tag), 1)), axis_tag, 0, 0), 0
+)
 
 
 def partner(x, axis, distance):
@@ -45,7 +48,7 @@
     guest = partner(outgoing, "dp", half_bit)
     paired_rows = place_block(tokens[:PAIR_ROWS], guest, kept_rows, PAIR_ROWS)
     dp_total, fsdp_total = (lax.axis_size("dp"), lax.axis_size("fsdp"))
-    sliced_rows = lax.all_to_all(paired_rows, "fsdp", split_axis=1, concat_axis=0, tiled=True)
+    sliced_rows = test_sides_over_axis(paired_rows, "fsdp")
     slice_width = sliced_rows.shape[1]
     all_rows = lax.all_gather(sliced_rows, "dp", axis=0, tiled=True)
     all_rows = all_rows.reshape(dp_total, fsdp_total, PAIR_ROWS, slice_width).swapaxes(0, 1)

time: 341 us -> 341 us (level)
  no operation moved by 1% of the time
where the time goes in v1:
time: 341 us; the launch traced here: 340 us
  waiting for transfers between devices  219 us (64%)
  blocking collectives  52.4 us (15%)
  matrix products  30 us (9%)
  local copies, waits for them, and re-layouts  19.3 us (6%)
  between operations  14.8 us (4%)
  starting transfers between devices  3.6 us (1%)
    reduce_scatter x1, waiting for transfers between devices, per_device(): lax.psum_scatter(partial_blocks, 'fsdp', scatter_dimension=0, tiled=True)  157 us
    ppermute x2, waiting for transfers between devices, partner(): lax.ppermute(x, axis, [(i, i ^ 1 << distance) for i in range(lax.axis_siz...  36.5 us
    all_to_all x1, blocking collectives, per_device(): lax.all_to_all(blocks, 'dp', split_axis=0, concat_axis=1, tiled=True)  31.4 us
    all_gather x1, waiting for transfers between devices, per_device(): all_rows = lax.all_gather(sliced_rows, 'dp', axis=0, tiled=True)  25.2 us
    all_to_all x1, blocking collectives, lax.all_to_all(jnp.stack(jnp.split(block_here, lax.axis_size(axis_tag), 1...  21 us
    dot_general x1, matrix products, per_device(): jnp.dot(all_rows.reshape(-1, slice_width), up_weight, preferred_element_t...  14.9 us
    dynamic_update_slice x2, local copies, waits for them, and re-layouts, place_block(): placed = lax.dynamic_update_slice_in_dim(padded, block, offset, 0)  11.3 us
    dot_general x1, matrix products, per_device(): jnp.dot(rank_projection, up_factor, preferred_element_type=jnp.float32)  8.18 us
  transfers between devices with their start and end apart: 4, of which 4 were waited for; matrix products, arithmetic and copies ran while one was open for 1% of the time, Pallas kernels for 0%

profile of v1, /device:TPU:0, one launch (start us, length us, event | category | flops | bytes accessed | tf_op | source)
XLA Modules:
  0.0 340.5 jit_solution(1763433905961873940)
XLA Ops:
  7.2 0.0 copy-start
  7.2 0.0 all-gather.2.cloned.1.call-start
  8.0 1.2 pad_dynamic-slice_fusion
  9.1 3.1 collective-permute-start
  12.2 1.4 broadcast_select_fusion
  13.6 7.7 %collective-permute-done = bf16[48,4096]{1,0:T(8,128)(2,1)S(1)} collective-permute-done((bf16[48,4096]{1,0:T(8,128)(2,1)S(1)}, bf16[48,4096]{1,0:T(8,128)(2,1)S(1)}, u32[]{:S(2)}, u32[]{:S(2)}) %collective-permute-start) | collective-permute-done | bytes 393248 | tf_op jit(solution)/shard_map/ppermute | solution.py:15
  21.3 2.3 dynamic_update_slice.6
  23.6 0.1 pad_maximum_fusion
  23.7 21.0 %all_to_all.24 = bf16[4,80,1024]{2,1,0:T(8,128)(2,1)} all-to-all(bf16[4,80,1024]{2,1,0:T(8,128)(2,1)S(1)} %pad_maximum_fusion), channel_id=1, replica_groups=mesh['groups'=2,'dp'=4,'fsdp'=4] {'fsdp'}, dimensions={0} | all-to-all | bytes 1310720 | tf_op jit(solution)/shard_map/all_to_all | solution.py:10
  44.7 0.0 all-gather.2.cloned.1.call-update
  44.7 0.0 reduce-scatter.2.cloned.1.call-start
  44.8 25.2 %all-gather.2.cloned.1.call-done = bf16[1280,1024]{1,0:T(8,128)(2,1)} async-done(((bf16[320,1024]{1,0:T(8,128)(2,1)}), bf16[1280,1024]{1,0:T(8,128)(2,1)}) %all-gather.2.cloned.1.call-update) | async-done | bytes 2621456 | tf_op jit(solution)/shard_map/all_gather | solution.py:53
  70.0 2.1 copy.11
  72.1 14.9 %convolution_convert_fusion = bf16[1280,3584]{1,0:T(8,128)(2,1)} fusion(bf16[1280,1024]{1,0:T(8,128)(2,1)S(1)} %bitcast.48, bf16[1024,3584]{1,0:T(8,128)(2,1)} %param.7), kind=kOutput, calls=%fused_computation.3 | convolution fusion | flops 9399828480 | bytes 19136512 | tf_op jit(solution)/shard_map/dot_general | solution.py:55
  86.9 0.0 reduce-scatter.2.cloned.1.call-update
  86.9 157.2 %reduce-scatter.2.cloned.1.call-done = bf16[320,3584]{1,0:T(8,128)(2,1)} async-done(((bf16[1280,3584]{1,0:T(8,128)(2,1)}), bf16[320,3584]{1,0:T(8,128)(2,1)}) %reduce-scatter.2.cloned.1.call-update) | async-done | bytes 2293776 | tf_op jit(solution)/shard_map/reduce_scatter | solution.py:58
  244.1 31.4 %all_to_all.25 = bf16[4,80,3584]{2,1,0:T(8,128)(2,1)S(1)} all-to-all(bf16[4,80,3584]{2,1,0:T(8,128)(2,1)} %bitcast.50), channel_id=1, replica_groups=mesh['groups'=2,'dp'=4,'fsdp'=4] {'dp'}, dimensions={0} | all-to-all | bytes 4587520 | tf_op jit(solution)/shard_map/all_to_all | solution.py:59
  275.5 0.0 copy-start.1
  275.5 0.0 copy-start.3
  275.5 0.2 copy.13
  275.7 0.4 pad_dynamic-slice_fusion.1
  276.2 0.5 collective-permute-start.1
  276.6 0.1 copy-done.1
  276.7 0.0 copy-done.3
  276.8 0.5 convolution_convert_fusion.1
  277.2 2.1 concatenate.12
  279.4 28.7 %collective-permute-done.1 = bf16[48,14336]{1,0:T(8,128)(2,1)S(1)} collective-permute-done((bf16[48,14336]{1,0:T(8,128)(2,1)S(1)}, bf16[48,14336]{1,0:T(8,128)(2,1)S(1)}, u32[]{:S(2)}, u32[]{:S(2)}) %collective-permute-start.1) | collective-permute-done | bytes 1376288 | tf_op jit(solution)/shard_map/ppermute | solution.py:15
  308.1 9.0 %dynamic_update_slice.7 = bf16[128,14336]{1,0:T(8,128)(2,1)} dynamic-update-slice(bf16[128,14336]{1,0:T(8,128)(2,1)} %concatenate.12, bf16[48,14336]{1,0:T(8,128)(2,1)S(1)} %collective-permute-done.1, s32[]{:T(128)S(6)} %select_n.16, s32[]{:T(128)} %constant.2.clone.1) | dynamic-update-slice | bytes 2752516 | tf_op jit(solution)/shard_map/dynamic_update_slice | solution.py:32
  317.1 0.0 copy-done
  317.1 8.2 %select_convert_fusion = (bf16[128,14336]{1,0:T(8,128)(2,1)S(1)}, bf16[128,14336]{1,0:T(8,128)(2,1)}) fusion(bf16[128,14336]{1,0:T(8,128)(2,1)} %param.11, bf16[128,14336]{1,0:T(8,128)(2,1)} %dynamic_update_slice.7, pred[128]{0:T(512)(128)(4,1)S(1)} %iota_compare_fusion, bf16[128,32]{0,1:T(8,128)(2,1)S(1)} %convolution_convert_fusion.1, ...), kind=kOutput, calls=%fused_computation.4 | convolution fusion | flops 148635648 | bytes 15605888 | tf_op jit(solution)/shard_map/dot_general | solution.py:65
  325.3 0.0 copy-start.2
  325.3 1.8 copy-done.2
  327.1 1.8 fusion
  329.0 4.6 %convolution_bitcast_fusion = f32[1,32,4096]{2,1,0:T(8,128)} fusion(bf16[128,4096]{1,0:T(8,128)(2,1)S(1)} %copy-done.1, bf16[128,14336]{1,0:T(8,128)(2,1)} %copy-done.2, bf16[1,32,14336]{2,1,0:T(8,128)(2,1)S(1)} %copy-done), kind=kOutput, calls=%fused_computation.8 | convolution fusion | flops 151003136 | bytes 6160384 | tf_op jit(solution)/shard_map/dot_general | solution.py:80
  (2 shorter events, 0.1 us)
Async XLA Ops:
  7.2 310.0 %copy-start = (bf16[1,32,14336]{2,1,0:T(8,128)(2,1)S(1)}, bf16[1,32,14336]{2,1,0:T(8,128)(2,1)}, u32[]{:S(2)}) copy-start(bf16[1,32,14336]{2,1,0:T(8,128)(2,1)} %param.9) | copy-start | bytes 2752516
  7.2 62.8 %all-gather.2.cloned.1.call-start = ((), (), s32[]{:S(2)}) async-start(), calls=%async_computation.3 | async-start | bytes 3276800 | tf_op jit(solution)/shard_map/all_gather | solution.py:53
  9.1 12.2 %collective-permute-start = (bf16[48,4096]{1,0:T(8,128)(2,1)S(1)}, bf16[48,4096]{1,0:T(8,128)(2,1)S(1)}, u32[]{:S(2)}, u32[]{:S(2)}) collective-permute-start(bf16[48,4096]{1,0:T(8,128)(2,1)S(1)} %pad_dynamic-slice_fusion), channel_id=1, source_target_pairs={{0,8},{4,12},{8,0},{12,4},{1,9},{5,13},{9,1},{13,5},{2,10},{6,14},... | collective-permute-start | bytes 1179656 | tf_op jit(solution)/shard_map/ppermute | solution.py:15
  44.7 199.4 %reduce-scatter.2.cloned.1.call-start = ((), (), s32[]{:S(2)}) async-start(), calls=%async_computation.4 | async-start | bytes 11468800 | tf_op jit(solution)/shard_map/reduce_scatter | solution.py:58
  275.5 1.2 copy-start.1
  275.5 1.3 copy-start.3
  276.2 31.9 %collective-permute-start.1 = (bf16[48,14336]{1,0:T(8,128)(2,1)S(1)}, bf16[48,14336]{1,0:T(8,128)(2,1)S(1)}, u32[]{:S(2)}, u32[]{:S(2)}) collective-permute-start(bf16[48,14336]{1,0:T(8,128)(2,1)S(1)} %pad_dynamic-slice_fusion.1), channel_id=1, source_target_pairs={{0,8},{4,12},{8,0},{12,4},{1,9},{5,13},{9,1},{13,5},{2,10},{6,14},... | collective-permute-start | bytes 4128776 | tf_op jit(solution)/shard_map/ppermute | solution.py:15
  325.3 1.8 copy-start.2
Sparse Core Ops, SparseCore 0:
  44.9 25.0 all-gather.1
  87.1 157.0 reduce-scatter.1
